TPU v7x, 32 devices: a whole 2x2x4 slice. The times are simulated.
32 devices in a mesh: groups: 2 (over y), vocab: 16 (over z, x, core).
Axes of the slice: x: 2, y: 2, z: 4, core: 2. Of those that a mesh axis runs over, the one named last changes fastest.
Arguments:
- hidden: bfloat16 [512, 1280], P(('groups', 'vocab')), parts along dimension 0, may hold values from -320 to 320
- embedding: bfloat16 [6144, 1280], P('vocab'), may hold values from -0.15625 to 0.15625
- prev_tokens: int32 [2, 512], P(None, 'groups'), parts along dimension 1, may hold values from 0 to 6143, as said below
- last_stamp: int32 [512], P('groups'), parts along dimension 0, may hold values from -1 to 1500, as said below
- sample_begin: int32 [512], P('groups'), parts along dimension 0, may hold values from 1 to 4
- seq_length: int32 [512], P('groups'), parts along dimension 0, may hold values from 1 to 9, as said below
- chosen: int32 [5, 512], P(None, 'groups'), parts along dimension 1, may hold values from 0 to 6143
Outputs:
- picked_logprob: float32 [5, 512], P(None, ('groups', 'vocab')), parts along dimension 1
- stamp_logprob: float32 [512], P(('groups', 'vocab')), parts along dimension 0
There are 2 independent parts, one for each index of `groups`. A program takes and returns all parts, laid end to end along the dimension named above; an argument that names none is the same for every part. Nothing has to cross between parts.
Inputs may be any that keep to these rules, and one draw needn't show every extreme that they name: prev_tokens[1, r] is row r's latest token and prev_tokens[0, r] the one before; ids at or above 4643 are timestamps. `last_stamp`: index among the 1501 timestamps of the latest timestamp token sampled since the row's sample begin, -1 if none; equal to the latest token's index when that token is a timestamp and was sampled. `seq_length`: at least the row's sample_begin and at most sample_begin + 5.
All inputs are finite; a program needn't handle non-finite values.
Results may differ from a plain program's by a relative error of at most 0.0003.
Values may be sent and summed in bfloat16 or wider, within the bound.
A program may use at most 64 MiB of HBM per device.

v0:
```python
import math

import jax
import jax.numpy as jnp
from jax import lax
from jax.sharding import PartitionSpec as P

TSN = 1501
SPECIALS = 108
INITIAL = 50


MASK_VALUE = -1000000000.0
EMPTY_VALUE = -3000000000.0
SLOPE = 4.0
FLOOR = -30.0


def rule_mask(columns, prev_tokens, last_stamp, sample_begin, seq_length, stamp_begin):
    generated = seq_length - sample_begin
    last_is = (generated >= 1) & (prev_tokens[1] >= stamp_begin)
    before_is = (generated < 2) | (prev_tokens[0] >= stamp_begin)
    column = columns[None, :]
    is_stamp = column >= stamp_begin
    offset = column - stamp_begin
    masked = column == stamp_begin - 1
    masked = masked | (last_is & before_is)[:, None] & is_stamp
    masked = masked | (last_is & ~before_is)[:, None] & (column < stamp_begin - SPECIALS)
    bound = last_stamp + jnp.where(last_is & ~before_is, 0, 1).astype(jnp.int32)
    masked = masked | is_stamp & (offset < bound[:, None]) & (last_stamp >= 0)[:, None]
    begin = (generated == 0)[:, None]
    masked = masked | begin & (column < stamp_begin)
    masked = masked | begin & is_stamp & (offset > INITIAL)
    return masked


def finalize(text_max, text_total, stamp_max, stamp_total, picked, chosen, stamp_begin):
    text_lse = text_max + jnp.log(text_total)
    stamp_lse = stamp_max + jnp.log(stamp_total)
    penalty = SLOPE * jnp.maximum(stamp_lse - text_max, 0.0)
    shifted = text_lse - penalty
    larger = jnp.maximum(shifted, stamp_lse)
    total = larger + jnp.log(jnp.exp(shifted - larger) + jnp.exp(stamp_lse - larger))
    adjusted = picked - jnp.where(chosen < stamp_begin, penalty[None, :], 0.0) - total[None, :]
    return (jnp.maximum(adjusted, FLOOR), jnp.maximum(stamp_lse - total, FLOOR))


def block_stats(
    rows, table, columns, is_text, prev, stamp, begin, length, local_pick, owned, stamp_begin
):
    logits = lax.dot_general(
        rows, table, (((1,), (1,)), ((), ())), preferred_element_type=jnp.float32
    )
    masked = rule_mask(columns, prev, stamp, begin, length, stamp_begin)
    values = jnp.where(masked, MASK_VALUE, logits)
    text_max = jnp.max(jnp.where(is_text, values, EMPTY_VALUE), axis=1)
    text_total = jnp.sum(jnp.where(is_text, jnp.exp(values - text_max[:, None]), 0.0), axis=1)
    stamp_max = jnp.max(jnp.where(is_text, EMPTY_VALUE, values), axis=1)
    stamp_total = jnp.sum(jnp.where(is_text, 0.0, jnp.exp(values - stamp_max[:, None])), axis=1)
    found = jnp.take_along_axis(values, local_pick.T, axis=1).T
    picked = jnp.where(owned, found, 0.0)
    return (text_max, text_total, stamp_max, stamp_total, picked)


def per_device(hidden, embedding, prev_tokens, last_stamp, sample_begin, seq_length, chosen):
    width = embedding.shape[0]
    row_dev = hidden.shape[0]
    count = lax.axis_size("vocab")
    index = lax.axis_index("vocab")
    stamp_begin = width * count - TSN
    first_column = index * width
    columns = first_column + lax.iota(jnp.int32, width)
    is_text = columns < stamp_begin
    nsel = chosen.shape[0]
    piece = lax.all_gather(hidden, "vocab", axis=0, tiled=True)
    rows_here = piece.shape[0]
    block = math.gcd(rows_here, 512)

    def one_block(number):
        begin_at = number * block
        inner = number * block
        pick = lax.dynamic_slice_in_dim(chosen, begin_at, block, 1)
        owned = (pick >= first_column) & (pick < first_column + width)
        local = jnp.clip(pick - first_column, 0, width - 1)
        result = block_stats(
            lax.dynamic_slice_in_dim(piece, inner, block, 0),
            embedding,
            columns,
            is_text,
            lax.dynamic_slice_in_dim(prev_tokens, begin_at, block, 1),
            lax.dynamic_slice_in_dim(last_stamp, begin_at, block, 0),
            lax.dynamic_slice_in_dim(sample_begin, begin_at, block, 0),
            lax.dynamic_slice_in_dim(seq_length, begin_at, block, 0),
            local,
            owned,
            stamp_begin,
        )
        return jnp.concatenate([jnp.stack(result[:4]), result[4]], axis=0)

    stacked = lax.map(one_block, jnp.arange(rows_here // block, dtype=jnp.int32))
    stats = jnp.transpose(stacked, (1, 0, 2)).reshape(4 + nsel, rows_here)
    text_max = stats[0]
    text_total = stats[1]
    stamp_max = stats[2]
    stamp_total = stats[3]
    picked = stats[4:]
    own = index * row_dev
    own_chosen = lax.dynamic_slice_in_dim(chosen, own, row_dev, 1)
    text_top, stamp_top = lax.pmax((text_max, stamp_max), "vocab")
    text_sum, stamp_sum = lax.psum(
        (text_total * jnp.exp(text_max - text_top), stamp_total * jnp.exp(stamp_max - stamp_top)),
        "vocab",
    )
    picked_own = lax.psum_scatter(picked, "vocab", scatter_dimension=1, tiled=True)
    text_own = lax.dynamic_slice_in_dim(text_top, own, row_dev, 0)
    text_sum_own = lax.dynamic_slice_in_dim(text_sum, own, row_dev, 0)
    stamp_own = lax.dynamic_slice_in_dim(stamp_top, own, row_dev, 0)
    stamp_sum_own = lax.dynamic_slice_in_dim(stamp_sum, own, row_dev, 0)
    return finalize(
        text_own, text_sum_own, stamp_own, stamp_sum_own, picked_own, own_chosen, stamp_begin
    )


def solution(mesh):
    placed = (
        P(("groups", "vocab"), None),
        P("vocab", None),
        P(None, "groups"),
        P("groups"),
        P("groups"),
        P("groups"),
        P(None, "groups"),
    )
    return jax.shard_map(
        per_device,
        mesh=mesh,
        in_specs=placed,
        out_specs=(P(None, ("groups", "vocab")), P(("groups", "vocab"))),
        check_vma=False,
    )
```

profile of v0, /device:TPU:0, one launch (start us, length us, event | category | flops | bytes accessed | tf_op | source)
XLA Modules:
  0.0 115.1 jit_solution(743491746212821573)
XLA Ops:
  7.2 0.0 copy-start
  7.2 0.0 reduce-scatter.4.cloned.1.call-start
  7.3 0.0 copy-start.3
  7.3 0.7 copy-done.3
  8.0 0.0 copy-start.1
  8.0 25.3 %all_gather.3 = bf16[256,1280]{1,0:T(8,128)(2,1)S(1)} all-gather(bf16[16,1280]{1,0:T(8,128)(2,1)} %param.7), channel_id=1, replica_groups=mesh['groups'=2,'vocab'=16] {'vocab'}, dimensions={0}, use_global_device_ids=true | all-gather | bytes 696320 | tf_op jit(solution)/shard_map/all_gather | solution.py:75
  33.4 0.0 copy-done.1
  33.4 0.1 copy.19
  33.5 0.0 copy-start.4
  33.6 0.0 copy-start.5
  33.6 0.2 reshape.60
  33.8 0.0 copy-start.2
  33.8 0.4 copy-done.4
  34.2 0.0 copy-done.5
  34.2 0.2 copy-done.2
  34.5 0.0 copy-done
  34.5 0.7 select_reduce_fusion.1
  35.2 10.1 %gather_fusion = f32[1280]{0:T(1024)S(1)} fusion(f32[256,384]{1,0:T(8,128)S(1)} %get-tuple-element.59, s32[1280]{0:T(1024)S(1)} %reshape.60), kind=kCustom, calls=%fused_computation | custom fusion | bytes 20480 | tf_op jit(solution)/shard_map/while/body/eval_jaxpr/jit(take_along_axis)/gather | solution.py:60
  45.3 0.2 reshape.63
  45.5 0.1 copy.20
  45.6 0.8 copy.21
  46.4 0.0 reduce-scatter.4.cloned.1.call-update
  46.4 29.8 %all-reduce.1 = (f32[256]{0:T(256)S(1)}, f32[256]{0:T(256)S(1)}) all-reduce(f32[256]{0:T(256)S(1)} %get-tuple-element.31, f32[256]{0:T(256)S(1)} %get-tuple-element.30), channel_id=1, replica_groups=mesh['groups'=2,'vocab'=16] {'vocab'}, use_global_device_ids=true, to_apply=%region_2.3 | all-reduce | flops 512 | bytes 4096 | tf_op jit(solution)/shard_map/pmax | solution.py:109
  76.3 0.3 select_reduce_fusion
  76.6 29.5 %all-reduce = (f32[256]{0:T(256)S(1)}, f32[256]{0:T(256)S(1)}) all-reduce(f32[256]{0:T(256)S(1)} %exponential_multiply_fusion.1, f32[256]{0:T(256)S(1)} %exponential_multiply_fusion), channel_id=1, replica_groups=mesh['groups'=2,'vocab'=16] {'vocab'}, use_global_device_ids=true, to_apply=%region_4.5 | all-reduce | flops 512 | bytes 4096 | tf_op jit(solution)/shard_map/psum | solution.py:110
  106.1 0.6 subtract_maximum_fusion.1
  106.7 0.1 maximum_multiply_fusion
  106.8 0.0 reduce-scatter.4.cloned.1.call-done
  106.8 0.8 copy.22
  107.6 0.7 subtract_maximum_fusion
  (11 shorter events, 0.1 us)
Async XLA Ops:
  7.2 27.3 %copy-start = (bf16[384,1280]{1,0:T(8,128)(2,1)S(1)}, bf16[384,1280]{1,0:T(8,128)(2,1)}, u32[]{:S(2)}) copy-start(bf16[384,1280]{1,0:T(8,128)(2,1)} %param.8) | copy-start | bytes 2949124
  7.2 99.6 %reduce-scatter.4.cloned.1.call-start = ((), (), s32[]{:S(2)}) async-start(), calls=%async_computation.1 | async-start | bytes 139264
  7.3 0.8 copy-start.3
  8.0 25.3 %copy-start.1 = (s32[5,256]{1,0:T(8,128)S(1)}, s32[5,256]{1,0:T(8,128)}, u32[]{:S(2)}) copy-start(s32[5,256]{1,0:T(8,128)} %param.13) | copy-start | bytes 15364
  33.5 0.7 copy-start.4
  33.6 0.7 copy-start.5
  33.8 0.7 copy-start.2
Sparse Core Ops, SparseCore 0:
  46.6 52.9 reduce-scatter.3
where the time goes:
time: 115 us
  blocking collectives  84.7 us (74%)
  between operations  14.2 us (12%)
  local copies, waits for them, and re-layouts  13.7 us (12%)
  other arithmetic  1.76 us (2%)
    pmax x1, blocking collectives, per_device(): text_top, stamp_top = lax.pmax((text_max, stamp_max), 'vocab')  29.8 us
    psum x1, blocking collectives, per_device(): lax.psum((text_total * jnp.exp(text_max - text_top), stamp_total * jnp.ex...  29.5 us
    all_gather x1, blocking collectives, per_device(): piece = lax.all_gather(hidden, 'vocab', axis=0, tiled=True)  25.3 us
    gather x5, local copies, waits for them, and re-layouts, block_stats(): found = jnp.take_along_axis(values, local_pick.T, axis=1).T  10.7 us
    unnamed x14, local copies, waits for them, and re-layouts  2.98 us
  transfers between devices with their start and end apart: 1, of which 0 were waited for; matrix products, arithmetic and copies ran while one was open for 1% of the time, Pallas kernels for 0%

commit v1 on v0

v1 whole, which is shorter than its diff:
```python
import functools
import math

import jax
import jax.numpy as jnp
from jax import lax
from jax.experimental import pallas as pl
from jax.experimental.pallas import tpu as pltpu
from jax.sharding import PartitionSpec as P

TSN = 1501
SPECIALS = 108
INITIAL = 50

MASK_VALUE = -1000000000.0
EMPTY_VALUE = -3000000000.0
SLOPE = 4.0
FLOOR = -30.0
BIG = 1 << 30
LANES = 128
MESH = pl.DeviceIdType.MESH


def kernel(
    count,
    hidden_ref,
    table_ref,
    prev_ref,
    stamp_ref,
    begin_ref,
    length_ref,
    chosen_ref,
    picked_ref,
    stamp_out_ref,
    rows_all,
    table,
    stats,
    gathered,
    table_sem,
    own_sem,
    send_sem,
    recv_sem,
    stat_send_sem,
    stat_recv_sem,
):
    row_dev = hidden_ref.shape[0]
    width = table_ref.shape[0]
    nsel = chosen_ref.shape[0]
    rows_here = count * row_dev
    stamp_begin = width * count - TSN
    group = lax.axis_index("groups")
    me = lax.axis_index("vocab")
    line = count // 4
    z, x, c = me // 4, (me // 2) % 2, me % 2

    def at(zz, xx, cc):
        return (zz * 2 + xx) * 2 + cc

    def slot(owner):
        return rows_all.at[pl.ds(pl.multiple_of(owner * row_dev, row_dev), row_dev)]

    load_own = pltpu.make_async_copy(hidden_ref, slot(me), own_sem)
    load_own.start()
    load_table = pltpu.make_async_copy(table_ref, table, table_sem)
    load_table.start()

    barrier = pltpu.get_barrier_semaphore()
    for i in range(1, count):
        pl.semaphore_signal(
            barrier, inc=1, device_id=(group, (me + i) % count), device_id_type=MESH
        )

    sends = []

    def send(owner, target):
        copy = pltpu.make_async_remote_copy(
            src_ref=slot(owner),
            dst_ref=slot(owner),
            send_sem=send_sem.at[len(sends)],
            recv_sem=recv_sem.at[owner],
            device_id=(group, target),
            device_id_type=MESH,
        )
        copy.start()
        sends.append(copy)

    def arrive(owner):
        pltpu.make_async_remote_copy(
            src_ref=slot(owner),
            dst_ref=slot(owner),
            send_sem=send_sem.at[0],
            recv_sem=recv_sem.at[owner],
            device_id=(group, (me + 1) % count),
            device_id_type=MESH,
        ).wait_recv()

    load_own.wait()
    pl.semaphore_wait(barrier, count - 1)
    order = sorted(range(1, line), key=lambda i: -min(i, line - i))
    across = at(z, 1 - x, c)
    partner = at(z, x, 1 - c)
    for i in order:
        send(me, at((z + i) % line, x, c))
    send(me, across)
    send(me, partner)
    for i in order:
        owner = at((z + line - i) % line, x, c)
        arrive(owner)
        send(owner, across)
        send(owner, partner)
    for i in [0] + order:
        owner = at((z + line - i) % line, 1 - x, c)
        arrive(owner)
        send(owner, partner)
    for i in [0] + order:
        arrive(at((z + line - i) % line, x, 1 - c))
    for i in [0] + order:
        arrive(at((z + line - i) % line, 1 - x, 1 - c))
    load_table.wait()

    block = math.gcd(rows_here, 256)
    column = me * width + lax.broadcasted_iota(jnp.int32, (width, block), 0)
    is_text = column < stamp_begin

    def one_block(number):
        at_row = number * block
        if not isinstance(number, int):
            at_row = pl.multiple_of(at_row, block)
        lanes = pl.ds(at_row, block)
        logits = lax.dot_general(
            table[...],
            rows_all[lanes, :],
            (((1,), (1,)), ((), ())),
            preferred_element_type=jnp.float32,
        )
        generated = length_ref[:, lanes] - begin_ref[:, lanes]
        last_stamp = stamp_ref[:, lanes]
        last_is = (generated >= 1) & (prev_ref[1:2, lanes] >= stamp_begin)
        before_is = (generated < 2) | (prev_ref[0:1, lanes] >= stamp_begin)
        opened = last_is & jnp.logical_not(before_is)
        closed = last_is & before_is
        first = generated == 0
        text_low = jnp.where(first, BIG, jnp.where(opened, stamp_begin - SPECIALS, 0))
        bound = last_stamp + jnp.where(opened, 0, 1)
        stamp_low = jnp.where(
            closed, BIG, stamp_begin + jnp.where(last_stamp >= 0, bound, 0)
        )
        stamp_high = jnp.where(first, stamp_begin + INITIAL + 1, BIG)
        low = jnp.where(is_text, text_low, stamp_low)
        high = jnp.where(is_text, stamp_begin - 1, stamp_high)
        values = jnp.where((column >= low) & (column < high), logits, MASK_VALUE)
        text_max = jnp.max(jnp.where(is_text, values, EMPTY_VALUE), axis=0, keepdims=True)
        stamp_max = jnp.max(jnp.where(is_text, EMPTY_VALUE, values), axis=0, keepdims=True)
        powers = jnp.exp(values - jnp.where(is_text, text_max, stamp_max))
        text_total = jnp.sum(jnp.where(is_text, powers, 0.0), axis=0, keepdims=True)
        stamp_total = jnp.sum(jnp.where(is_text, 0.0, powers), axis=0, keepdims=True)
        text_lse = jnp.where(text_total > 0.0, text_max + jnp.log(text_total), EMPTY_VALUE)
        stamp_lse = jnp.where(stamp_total > 0.0, stamp_max + jnp.log(stamp_total), EMPTY_VALUE)
        found = [
            jnp.sum(
                jnp.where(column == chosen_ref[k : k + 1, lanes], values, 0.0),
                axis=0,
                keepdims=True,
            )
            for k in range(nsel)
        ]
        lines = [text_max, text_lse, stamp_lse] + found
        lines += [jnp.zeros_like(text_max)] * (8 - len(lines))
        result = jnp.concatenate(lines, axis=0)
        for part in range(block // LANES):
            stats[number * (block // LANES) + part] = result[:, part * LANES : (part + 1) * LANES]

    if rows_here == block:
        one_block(0)
    else:
        pl.loop(0, rows_here // block)(one_block)

    def stat_copy(i):
        target = (me + i) % count
        return pltpu.make_async_remote_copy(
            src_ref=stats.at[(target * row_dev) // LANES],
            dst_ref=gathered.at[me],
            send_sem=stat_send_sem.at[i],
            recv_sem=stat_recv_sem.at[me],
            device_id=(group, target),
            device_id_type=MESH,
        )

    stat_sends = [stat_copy(i) for i in range(1, count)]
    for copy in stat_sends:
        copy.start()
    chunk = (me * row_dev) // LANES
    gathered[me] = stats[chunk]
    for copy in sends:
        copy.wait_send()
    for i in range(1, count):
        source = (me + count - i) % count
        pltpu.make_async_remote_copy(
            src_ref=stats.at[0],
            dst_ref=gathered.at[source],
            send_sem=stat_send_sem.at[0],
            recv_sem=stat_recv_sem.at[source],
            device_id=(group, (me + 1) % count),
            device_id_type=MESH,
        ).wait_recv()

    tiles = gathered[...]
    top = jnp.max(tiles, axis=0)
    lse = top + jnp.log(jnp.sum(jnp.exp(tiles - top[None]), axis=0))
    picked = jnp.sum(tiles, axis=0)[3 : 3 + nsel]
    text_max, text_lse, stamp_lse = top[0:1], lse[1:2], lse[2:3]
    penalty = SLOPE * jnp.maximum(stamp_lse - text_max, 0.0)
    shifted = text_lse - penalty
    larger = jnp.maximum(shifted, stamp_lse)
    total = larger + jnp.log(jnp.exp(shifted - larger) + jnp.exp(stamp_lse - larger))
    own_chosen = chosen_ref[:, pl.ds(pl.multiple_of(chunk * LANES, LANES), LANES)]
    adjusted = picked - jnp.where(own_chosen < stamp_begin, penalty, 0.0) - total
    final = jnp.concatenate(
        [adjusted, stamp_lse - total] + [jnp.zeros_like(total)] * (7 - nsel), axis=0
    )
    final = jnp.maximum(final, FLOOR)
    offset = (me * row_dev) % LANES
    final = pltpu.roll(final, (LANES - offset) % LANES, 1)
    picked_ref[...] = final[:nsel, :row_dev]
    stamp_out_ref[...] = final[nsel : nsel + 1, :row_dev]
    for copy in stat_sends:
        copy.wait_send()


def per_device(hidden, embedding, prev_tokens, last_stamp, sample_begin, seq_length, chosen):
    count = lax.axis_size("vocab")
    row_dev, depth = hidden.shape
    width = embedding.shape[0]
    nsel = chosen.shape[0]
    rows_here = count * row_dev
    anywhere = pl.BlockSpec(memory_space=pl.ANY)
    local = pl.BlockSpec(memory_space=pltpu.VMEM)
    picked, stamp = pl.pallas_call(
        functools.partial(kernel, count),
        out_shape=(
            jax.ShapeDtypeStruct((nsel, row_dev), jnp.float32),
            jax.ShapeDtypeStruct((1, row_dev), jnp.float32),
        ),
        in_specs=[anywhere, anywhere] + [local] * 5,
        out_specs=(local, local),
        scratch_shapes=[
            pltpu.VMEM((rows_here, depth), hidden.dtype),
            pltpu.VMEM((width, depth), embedding.dtype),
            pltpu.VMEM((rows_here // LANES, 8, LANES), jnp.float32),
            pltpu.VMEM((count, 8, LANES), jnp.float32),
            pltpu.SemaphoreType.DMA,
            pltpu.SemaphoreType.DMA,
            pltpu.SemaphoreType.DMA((count,)),
            pltpu.SemaphoreType.DMA((count,)),
            pltpu.SemaphoreType.DMA((count,)),
            pltpu.SemaphoreType.DMA((count,)),
        ],
        compiler_params=pltpu.CompilerParams(collective_id=0, has_side_effects=True),
        name="decode_step",
    )(
        hidden,
        embedding,
        prev_tokens,
        last_stamp[None, :],
        sample_begin[None, :],
        seq_length[None, :],
        chosen,
    )
    return picked, stamp[0]


def solution(mesh):
    placed = (
        P(("groups", "vocab"), None),
        P("vocab", None),
        P(None, "groups"),
        P("groups"),
        P("groups"),
        P("groups"),
        P(None, "groups"),
    )
    return jax.shard_map(
        per_device,
        mesh=mesh,
        in_specs=placed,
        out_specs=(P(None, ("groups", "vocab")), P(("groups", "vocab"))),
        check_vma=False,
    )
```

time: 115 us -> 24.8 us (0.22)
  blocking collectives: 84.7 us -> 0 us
  Pallas kernels: 0 us -> 22.1 us
  between operations: 14.2 us -> 0.65 us
  local copies, waits for them, and re-layouts: 13.7 us -> 1.82 us
  other arithmetic: 1.76 us -> 0 us
    pmax x1 -> x0, blocking collectives: 29.8 us -> none  [per_device(): text_top, stamp_top = lax.pmax((text_max, stamp_max), 'vocab')]
    psum x1 -> x0, blocking collectives: 29.5 us -> none  [per_device(): lax.psum((text_total * jnp.exp(text_max - text_top), stamp_total * jnp.ex...]
    all_gather x1 -> x0, blocking collectives: 25.3 us -> none  [per_device(): piece = lax.all_gather(hidden, 'vocab', axis=0, tiled=True)]
    pallas_call x0 -> x1, Pallas kernels: none -> 22.1 us  [per_device(): pl.pallas_call(functools.partial(kernel, count), out_shape=(jax.ShapeDtyp...]
    gather x5 -> x0, local copies, waits for them, and re-layouts: 10.7 us -> none  [block_stats(): found = jnp.take_along_axis(values, local_pick.T, axis=1).T]
    max x2 -> x0, other arithmetic: 1.29 us -> none  [finalize(): return (jnp.maximum(adjusted, FLOOR), jnp.maximum(stamp_lse - total, FLOOR))]
    unnamed x14 -> x6, local copies, waits for them, and re-layouts: 2.98 us -> 1.82 us
  transfers between devices with their start and end apart: 1 -> 0, of which waited for: 0 -> 0; matrix products, arithmetic and copies ran while one was open for 1% -> 0% of each run, Pallas kernels for 0% -> 0%
where the time goes in v1:
time: 24.8 us; the launch traced here: 24.5 us
  Pallas kernels  22.1 us (89%)
  local copies, waits for them, and re-layouts  1.82 us (7%)
  between operations  0.65 us (3%)
    pallas_call x1, Pallas kernels, per_device(): pl.pallas_call(functools.partial(kernel, count), out_shape=(jax.ShapeDtyp...  22.1 us
    unnamed x6, local copies, waits for them, and re-layouts  1.82 us

profile of v1, /device:TPU:0, one launch (start us, length us, event | category | flops | bytes accessed | tf_op | source)
XLA Modules:
  0.0 24.5 jit_solution(12350772919853883851)
XLA Ops:
  0.6 22.1 %decode_step.1 = (f32[5,16]{1,0:T(8,128)}, f32[1,16]{1,0:T(1,128)}) custom-call(bf16[16,1280]{1,0:T(8,128)(2,1)} %hidden_ref.1, bf16[384,1280]{1,0:T(8,128)(2,1)} %table_ref.1, s32[2,256]{1,0:T(2,128)} %prev_ref.1, s32[1,256]{1,0:T(1,128)} %bitcast.4, s32[1,256]{1,0:T(1,128)} %bitcast.5, s32[1,256]{1,0:T(1,128)} %bitcast.6, s32[5,256]{1,0:T(8,128)} %chosen_ref.1), custom_call_target="tpu_custom_call" | custom-call | tf_op jit(solution)/shard_map/decode_step/pallas_call | solution.py:238
  22.7 0.0 copy-start
  22.7 0.7 %copy-done = f32[5,16]{1,0:T(8,128)S(1)} copy-done((f32[5,16]{1,0:T(8,128)S(1)}, f32[5,16]{1,0:T(8,128)}, u32[]{:S(2)}) %copy-start) | copy-done | bytes 344
  23.4 0.0 copy-start.1
  23.4 0.6 %copy.11 = f32[5,16]{1,0:T(8,128)} copy(f32[5,16]{1,0:T(8,128)S(1)} %copy-done) | data formatting | bytes 640
  24.0 0.0 copy-done.1
  24.0 0.5 %copy.12 = f32[16]{0:T(128)} copy(f32[16]{0:T(128)S(1)} %bitcast.7) | data formatting | bytes 128
Async XLA Ops:
  22.7 0.7 %copy-start = (f32[5,16]{1,0:T(8,128)S(1)}, f32[5,16]{1,0:T(8,128)}, u32[]{:S(2)}) copy-start(f32[5,16]{1,0:T(8,128)} %get-tuple-element.8) | copy-start | bytes 964
  23.4 0.6 %copy-start.1 = (f32[1,16]{1,0:T(1,128)S(1)}, f32[1,16]{1,0:T(1,128)}, u32[]{:S(2)}) copy-start(f32[1,16]{1,0:T(1,128)} %get-tuple-element.5) | copy-start | bytes 196

commit v2 on v1

v2 whole, which is shorter than its diff:
```python
import functools

import jax
import jax.numpy as jnp
from jax import lax
from jax.experimental import pallas as pl
from jax.experimental.pallas import tpu as pltpu
from jax.sharding import PartitionSpec as P

TSN = 1501
SPECIALS = 108
INITIAL = 50

MASK_VALUE = -1000000000.0
EMPTY_VALUE = -3000000000.0
SLOPE = 4.0
FLOOR = -30.0
BIG = 1 << 30
LANES = 128
MESH = pl.DeviceIdType.MESH


def kernel(
    count,
    hidden_ref,
    table_ref,
    prev_ref,
    stamp_ref,
    begin_ref,
    length_ref,
    chosen_ref,
    picked_ref,
    stamp_out_ref,
    rows_all,
    table,
    prev_in,
    stamp_in,
    begin_in,
    length_in,
    chosen_in,
    ordered,
    stats,
    gathered,
    load_sem,
    table_send_sem,
    table_recv_sem,
    send_sem,
    recv_sem,
    stat_send_sem,
    stat_recv_sem,
):
    row_dev = hidden_ref.shape[0]
    width = table_ref.shape[0]
    nsel = chosen_ref.shape[0]
    chips = count // 2
    line = chips // 2
    rows_half = chips * row_dev
    stamp_begin = width * count - TSN
    group = lax.axis_index("groups")
    me = lax.axis_index("vocab")
    chip, core = me // 2, me % 2
    z, x = chip // 2, chip % 2

    def slot(owner):
        return rows_all.at[pl.ds(pl.multiple_of(owner * row_dev, row_dev), row_dev)]

    def half(which):
        return table.at[pl.ds(pl.multiple_of(which * width, width), width)]

    load_own = pltpu.make_async_copy(hidden_ref, slot(chip), load_sem.at[0])
    load_own.start()
    small = [
        pltpu.make_async_copy(source, target, load_sem.at[2 + i])
        for i, (source, target) in enumerate(
            [
                (prev_ref, prev_in),
                (stamp_ref, stamp_in),
                (begin_ref, begin_in),
                (length_ref, length_in),
                (chosen_ref, chosen_in),
            ]
        )
    ]
    for copy in small:
        copy.start()
    load_table = pltpu.make_async_copy(table_ref, half(core), load_sem.at[1])
    load_table.start()

    barrier = pltpu.get_barrier_semaphore()
    for i in range(1, chips):
        pl.semaphore_signal(
            barrier,
            inc=1,
            device_id=(group, ((chip + i) % chips) * 2 + core),
            device_id_type=MESH,
        )
    partner = chip * 2 + 1 - core
    pl.semaphore_signal(barrier, inc=1, device_id=(group, partner), device_id_type=MESH)

    sends = []

    def send(owner, target):
        copy = pltpu.make_async_remote_copy(
            src_ref=slot(owner),
            dst_ref=slot(owner),
            send_sem=send_sem.at[len(sends)],
            recv_sem=recv_sem.at[owner],
            device_id=(group, target * 2 + core),
            device_id_type=MESH,
        )
        copy.start()
        sends.append(copy)

    def arrive(owner):
        pltpu.make_async_remote_copy(
            src_ref=slot(owner),
            dst_ref=slot(owner),
            send_sem=send_sem.at[0],
            recv_sem=recv_sem.at[owner],
            device_id=(group, partner),
            device_id_type=MESH,
        ).wait_recv()

    load_own.wait()
    pl.semaphore_wait(barrier, chips)
    sign = 1 - 2 * ((2 * z) // line)
    across = z * 2 + 1 - x
    order = list(range(line - 1, 0, -1))
    for i in order:
        send(chip, ((z + sign * i + line) % line) * 2 + x)
    send(chip, across)
    share = pltpu.make_async_remote_copy(
        src_ref=table_ref,
        dst_ref=half(core),
        send_sem=table_send_sem,
        recv_sem=table_recv_sem,
        device_id=(group, partner),
        device_id_type=MESH,
    )
    share.start()

    for copy in small:
        copy.wait()
    lane_from = lax.broadcasted_iota(jnp.int32, (2 * LANES, LANES), 0)
    lane_to = lax.broadcasted_iota(jnp.int32, (2 * LANES, LANES), 1)
    wanted = (lane_to // row_dev * 2 + core) * row_dev + lane_to % row_dev
    select = jnp.where(lane_from == wanted, 1.0, 0.0)
    for number in range(rows_half // LANES):
        lanes = pl.ds(number * 2 * LANES, 2 * LANES)
        stacked = jnp.concatenate(
            [
                prev_in[:, lanes],
                stamp_in[:, lanes],
                begin_in[:, lanes],
                length_in[:, lanes],
                chosen_in[:, lanes],
                jnp.zeros((16 - 5 - nsel, 2 * LANES), jnp.int32),
            ],
            axis=0,
        )
        ordered[number] = lax.dot_general(
            stacked.astype(jnp.float32),
            select,
            (((1,), (0,)), ((), ())),
            precision=lax.Precision.HIGHEST,
            preferred_element_type=jnp.float32,
        ).astype(jnp.int32)

    for i in order:
        owner = ((z - sign * i + 2 * line) % line) * 2 + x
        arrive(owner)
        send(owner, across)
    load_table.wait()
    share.wait_recv()
    for i in [0] + order:
        arrive(((z - sign * i + 2 * line) % line) * 2 + 1 - x)

    column = chip * 2 * width + lax.broadcasted_iota(jnp.int32, (2 * width, LANES), 0)
    is_text = column < stamp_begin

    def one_block(number):
        at_row = number * LANES
        if not isinstance(number, int):
            at_row = pl.multiple_of(at_row, LANES)
        logits = lax.dot_general(
            table[...],
            rows_all[pl.ds(at_row, LANES), :],
            (((1,), (1,)), ((), ())),
            preferred_element_type=jnp.float32,
        )
        row = ordered[number]
        generated = row[4:5] - row[3:4]
        last_stamp = row[2:3]
        last_is = (generated >= 1) & (row[1:2] >= stamp_begin)
        before_is = (generated < 2) | (row[0:1] >= stamp_begin)
        opened = last_is & jnp.logical_not(before_is)
        closed = last_is & before_is
        first = generated == 0
        text_low = jnp.where(first, BIG, jnp.where(opened, stamp_begin - SPECIALS, 0))
        bound = last_stamp + jnp.where(opened, 0, 1)
        stamp_low = jnp.where(
            closed, BIG, stamp_begin + jnp.where(last_stamp >= 0, bound, 0)
        )
        stamp_high = jnp.where(first, stamp_begin + INITIAL + 1, BIG)
        low = jnp.where(is_text, text_low, stamp_low)
        high = jnp.where(is_text, stamp_begin - 1, stamp_high)
        values = jnp.where((column >= low) & (column < high), logits, MASK_VALUE)
        text_max = jnp.max(jnp.where(is_text, values, EMPTY_VALUE), axis=0, keepdims=True)
        stamp_max = jnp.max(jnp.where(is_text, EMPTY_VALUE, values), axis=0, keepdims=True)
        powers = jnp.exp(values - jnp.where(is_text, text_max, stamp_max))
        text_total = jnp.sum(jnp.where(is_text, powers, 0.0), axis=0, keepdims=True)
        stamp_total = jnp.sum(jnp.where(is_text, 0.0, powers), axis=0, keepdims=True)
        text_lse = jnp.where(text_total > 0.0, text_max + jnp.log(text_total), EMPTY_VALUE)
        stamp_lse = jnp.where(stamp_total > 0.0, stamp_max + jnp.log(stamp_total), EMPTY_VALUE)
        found = [
            jnp.sum(
                jnp.where(column == row[5 + k : 6 + k], values, 0.0), axis=0, keepdims=True
            )
            for k in range(nsel)
        ]
        lines = [text_max, text_lse, stamp_lse] + found
        lines += [jnp.zeros_like(text_max)] * (8 - len(lines))
        stats[number] = jnp.concatenate(lines, axis=0)

    if rows_half == LANES:
        one_block(0)
    else:
        pl.loop(0, rows_half // LANES)(one_block)

    def stat_copy(i):
        target = (chip + i) % chips
        return pltpu.make_async_remote_copy(
            src_ref=stats.at[(target * row_dev) // LANES],
            dst_ref=gathered.at[chip],
            send_sem=stat_send_sem.at[i],
            recv_sem=stat_recv_sem.at[chip],
            device_id=(group, target * 2 + core),
            device_id_type=MESH,
        )

    stat_sends = [stat_copy(i) for i in range(1, chips)]
    for copy in stat_sends:
        copy.start()
    piece = (chip * row_dev) // LANES
    gathered[chip] = stats[piece]
    for copy in sends:
        copy.wait_send()
    share.wait_send()
    for i in range(1, chips):
        source = (chip + chips - i) % chips
        pltpu.make_async_remote_copy(
            src_ref=stats.at[0],
            dst_ref=gathered.at[source],
            send_sem=stat_send_sem.at[0],
            recv_sem=stat_recv_sem.at[source],
            device_id=(group, partner),
            device_id_type=MESH,
        ).wait_recv()

    tiles = gathered[...]
    top = jnp.max(tiles, axis=0)
    lse = top + jnp.log(jnp.sum(jnp.exp(tiles - top[None]), axis=0))
    picked = jnp.sum(tiles, axis=0)[3 : 3 + nsel]
    text_max, text_lse, stamp_lse = top[0:1], lse[1:2], lse[2:3]
    penalty = SLOPE * jnp.maximum(stamp_lse - text_max, 0.0)
    shifted = text_lse - penalty
    larger = jnp.maximum(shifted, stamp_lse)
    total = larger + jnp.log(jnp.exp(shifted - larger) + jnp.exp(stamp_lse - larger))
    own_chosen = ordered[piece][5 : 5 + nsel]
    adjusted = picked - jnp.where(own_chosen < stamp_begin, penalty, 0.0) - total
    final = jnp.concatenate(
        [adjusted, stamp_lse - total] + [jnp.zeros_like(total)] * (7 - nsel), axis=0
    )
    final = jnp.maximum(final, FLOOR)
    offset = (chip * row_dev) % LANES
    final = pltpu.roll(final, (LANES - offset) % LANES, 1)
    picked_ref[...] = final[:nsel, :row_dev]
    stamp_out_ref[...] = final[nsel : nsel + 1, :row_dev]
    for copy in stat_sends:
        copy.wait_send()


def per_device(hidden, embedding, prev_tokens, last_stamp, sample_begin, seq_length, chosen):
    count = lax.axis_size("vocab")
    row_dev, depth = hidden.shape
    width = embedding.shape[0]
    nsel = chosen.shape[0]
    chips = count // 2
    rows_here = count * row_dev
    rows_half = chips * row_dev
    anywhere = pl.BlockSpec(memory_space=pl.ANY)
    local = pl.BlockSpec(memory_space=pltpu.VMEM)
    picked, stamp = pl.pallas_call(
        functools.partial(kernel, count),
        out_shape=(
            pltpu.VMEM((nsel, row_dev), jnp.float32),
            pltpu.VMEM((1, row_dev), jnp.float32),
        ),
        in_specs=[anywhere] * 7,
        out_specs=(local, local),
        scratch_shapes=[
            pltpu.VMEM((rows_half, depth), hidden.dtype),
            pltpu.VMEM((2 * width, depth), embedding.dtype),
            pltpu.VMEM((2, rows_here), jnp.int32),
            pltpu.VMEM((1, rows_here), jnp.int32),
            pltpu.VMEM((1, rows_here), jnp.int32),
            pltpu.VMEM((1, rows_here), jnp.int32),
            pltpu.VMEM((nsel, rows_here), jnp.int32),
            pltpu.VMEM((rows_half // LANES, 16, LANES), jnp.int32),
            pltpu.VMEM((rows_half // LANES, 8, LANES), jnp.float32),
            pltpu.VMEM((chips, 8, LANES), jnp.float32),
            pltpu.SemaphoreType.DMA((7,)),
            pltpu.SemaphoreType.DMA,
            pltpu.SemaphoreType.DMA,
            pltpu.SemaphoreType.DMA((chips,)),
            pltpu.SemaphoreType.DMA((chips,)),
            pltpu.SemaphoreType.DMA((chips,)),
            pltpu.SemaphoreType.DMA((chips,)),
        ],
        compiler_params=pltpu.CompilerParams(collective_id=0, has_side_effects=True),
        name="decode_step",
    )(
        hidden,
        embedding,
        prev_tokens,
        last_stamp[None, :],
        sample_begin[None, :],
        seq_length[None, :],
        chosen,
    )
    return picked, stamp[0]


def solution(mesh):
    placed = (
        P(("groups", "vocab"), None),
        P("vocab", None),
        P(None, "groups"),
        P("groups"),
        P("groups"),
        P("groups"),
        P(None, "groups"),
    )
    return jax.shard_map(
        per_device,
        mesh=mesh,
        in_specs=placed,
        out_specs=(P(None, ("groups", "vocab")), P(("groups", "vocab"))),
        check_vma=False,
    )
```

time: 24.8 us -> 21.6 us (0.87)
  Pallas kernels: 22.1 us -> 19.7 us
  local copies, waits for them, and re-layouts: 1.82 us -> 1.11 us
    pallas_call x1, Pallas kernels: 22.1 us -> 19.7 us  [per_device(): pl.pallas_call(functools.partial(kernel, count), out_shape=(pltpu.VMEM((n...]
    unnamed x6 -> x2, local copies, waits for them, and re-layouts: 1.82 us -> 1.11 us
where the time goes in v2:
time: 21.6 us; the launch traced here: 21.4 us
  Pallas kernels  19.7 us (91%)
  local copies, waits for them, and re-layouts  1.11 us (5%)
  between operations  0.64 us (3%)
    pallas_call x1, Pallas kernels, per_device(): pl.pallas_call(functools.partial(kernel, count), out_shape=(pltpu.VMEM((n...  19.7 us
    unnamed x2, local copies, waits for them, and re-layouts  1.11 us

profile of v2, /device:TPU:0, one launch (start us, length us, event | category | flops | bytes accessed | tf_op | source)
XLA Modules:
  0.0 21.4 jit_solution(13712364925289314884)
XLA Ops:
  0.6 19.7 %decode_step.1 = (f32[5,16]{1,0:T(8,128)S(1)}, f32[1,16]{1,0:T(1,128)S(1)}) custom-call(bf16[16,1280]{1,0:T(8,128)(2,1)} %hidden_ref.1, bf16[384,1280]{1,0:T(8,128)(2,1)} %table_ref.1, s32[2,256]{1,0:T(2,128)} %prev_ref.1, s32[1,256]{1,0:T(1,128)} %bitcast.5, s32[1,256]{1,0:T(1,128)} %bitcast.6, s32[1,256]{1,0:T(1,128)} %bitcast.7, s32[5,256]{1,0:T(8,128)} %chosen_ref.1), custom_call_target="tpu_custom_call" | custom-call | tf_op jit(solution)/shard_map/decode_step/pallas_call | solution.py:293
  20.3 0.6 %copy.11 = f32[5,16]{1,0:T(8,128)} copy(f32[5,16]{1,0:T(8,128)S(1)} %get-tuple-element.6) | data formatting | bytes 640
  20.9 0.5 %copy.12 = f32[16]{0:T(128)} copy(f32[16]{0:T(128)S(1)} %bitcast.4) | data formatting | bytes 128

commit v3 on v2

--- a/solution.py
+++ b/solution.py
@@ -61,13 +61,19 @@
     chip, core = me // 2, me % 2
     z, x = chip // 2, chip % 2
 
-    def slot(owner):
-        return rows_all.at[pl.ds(pl.multiple_of(owner * row_dev, row_dev), row_dev)]
+    parts = recv_sem.shape[1]
+    cut = rows_all.shape[1] // parts
+
+    def slot(owner, part):
+        return rows_all.at[
+            pl.ds(pl.multiple_of(owner * row_dev, row_dev), row_dev),
+            pl.ds(part * cut, cut),
+        ]
 
     def half(which):
         return table.at[pl.ds(pl.multiple_of(which * width, width), width)]
 
-    load_own = pltpu.make_async_copy(hidden_ref, slot(chip), load_sem.at[0])
+    load_own = pltpu.make_async_copy(hidden_ref, rows_all.at[pl.ds(pl.multiple_of(chip * row_dev, row_dev), row_dev)], load_sem.at[0])
     load_own.start()
     small = [
         pltpu.make_async_copy(source, target, load_sem.at[2 + i])
@@ -87,48 +93,45 @@
     load_table.start()
 
     barrier = pltpu.get_barrier_semaphore()
-    for i in range(1, chips):
-        pl.semaphore_signal(
-            barrier,
-            inc=1,
-            device_id=(group, ((chip + i) % chips) * 2 + core),
-            device_id_type=MESH,
-        )
+    across = z * 2 + 1 - x
     partner = chip * 2 + 1 - core
-    pl.semaphore_signal(barrier, inc=1, device_id=(group, partner), device_id_type=MESH)
+    greeted = [(((z + i) % line) * 2 + x) * 2 + core for i in range(1, line)]
+    greeted += [across * 2 + core, partner]
+    for peer in greeted:
+        pl.semaphore_signal(barrier, inc=1, device_id=(group, peer), device_id_type=MESH)
 
     sends = []
 
-    def send(owner, target):
+    def send(owner, part, target):
         copy = pltpu.make_async_remote_copy(
-            src_ref=slot(owner),
-            dst_ref=slot(owner),
+            src_ref=slot(owner, part),
+            dst_ref=slot(owner, part),
             send_sem=send_sem.at[len(sends)],
-            recv_sem=recv_sem.at[owner],
+            recv_sem=recv_sem.at[owner, part],
             device_id=(group, target * 2 + core),
             device_id_type=MESH,
         )
         copy.start()
         sends.append(copy)
 
-    def arrive(owner):
+    def arrive(owner, part):
         pltpu.make_async_remote_copy(
-            src_ref=slot(owner),
-            dst_ref=slot(owner),
+            src_ref=slot(owner, part),
+            dst_ref=slot(owner, part),
             send_sem=send_sem.at[0],
-            recv_sem=recv_sem.at[owner],
+            recv_sem=recv_sem.at[owner, part],
             device_id=(group, partner),
             device_id_type=MESH,
         ).wait_recv()
 
     load_own.wait()
-    pl.semaphore_wait(barrier, chips)
+    pl.semaphore_wait(barrier, len(greeted))
     sign = 1 - 2 * ((2 * z) // line)
-    across = z * 2 + 1 - x
     order = list(range(line - 1, 0, -1))
-    for i in order:
-        send(chip, ((z + sign * i + line) % line) * 2 + x)
-    send(chip, across)
+    for part in range(parts):
+        for i in order:
+            send(chip, part, ((z + sign * i + line) % line) * 2 + x)
+        send(chip, part, across)
     share = pltpu.make_async_remote_copy(
         src_ref=table_ref,
         dst_ref=half(core),
@@ -166,14 +169,16 @@
             preferred_element_type=jnp.float32,
         ).astype(jnp.int32)
 
-    for i in order:
-        owner = ((z - sign * i + 2 * line) % line) * 2 + x
-        arrive(owner)
-        send(owner, across)
+    for part in range(parts):
+        for i in order:
+            owner = ((z - sign * i + 2 * line) % line) * 2 + x
+            arrive(owner, part)
+            send(owner, part, across)
     load_table.wait()
     share.wait_recv()
-    for i in [0] + order:
-        arrive(((z - sign * i + 2 * line) % line) * 2 + 1 - x)
+    for part in range(parts):
+        for i in [0] + order:
+            arrive(((z - sign * i + 2 * line) % line) * 2 + 1 - x, part)
 
     column = chip * 2 * width + lax.broadcasted_iota(jnp.int32, (2 * width, LANES), 0)
     is_text = column < stamp_begin
@@ -228,7 +233,7 @@
         pl.loop(0, rows_half // LANES)(one_block)
 
     def stat_copy(i):
-        target = (chip + i) % chips
+        target = (chip + sign * i + chips) % chips
         return pltpu.make_async_remote_copy(
             src_ref=stats.at[(target * row_dev) // LANES],
             dst_ref=gathered.at[chip],
@@ -238,7 +243,7 @@
             device_id_type=MESH,
         )
 
-    stat_sends = [stat_copy(i) for i in range(1, chips)]
+    stat_sends = [stat_copy(i) for i in range(chips - 1, 0, -1)]
     for copy in stat_sends:
         copy.start()
     piece = (chip * row_dev) // LANES
@@ -288,6 +293,7 @@
     chips = count // 2
     rows_here = count * row_dev
     rows_half = chips * row_dev
+    parts = 2 if depth % (2 * LANES) == 0 else 1
     anywhere = pl.BlockSpec(memory_space=pl.ANY)
     local = pl.BlockSpec(memory_space=pltpu.VMEM)
     picked, stamp = pl.pallas_call(
@@ -312,8 +318,8 @@
             pltpu.SemaphoreType.DMA((7,)),
             pltpu.SemaphoreType.DMA,
             pltpu.SemaphoreType.DMA,
-            pltpu.SemaphoreType.DMA((chips,)),
-            pltpu.SemaphoreType.DMA((chips,)),
+            pltpu.SemaphoreType.DMA((chips * parts,)),
+            pltpu.SemaphoreType.DMA((chips, parts)),
             pltpu.SemaphoreType.DMA((chips,)),
             pltpu.SemaphoreType.DMA((chips,)),
         ],

time: 21.6 us -> 20.1 us (0.931)
  Pallas kernels: 19.7 us -> 18.2 us
    pallas_call x1, Pallas kernels: 19.7 us -> 18.2 us  [per_device(): pl.pallas_call(functools.partial(kernel, count), out_shape=(pltpu.VMEM((n...]
where the time goes in v3:
time: 20.1 us; the launch traced here: 20 us
  Pallas kernels  18.2 us (91%)
  local copies, waits for them, and re-layouts  1.11 us (6%)
  between operations  0.64 us (3%)
    pallas_call x1, Pallas kernels, per_device(): pl.pallas_call(functools.partial(kernel, count), out_shape=(pltpu.VMEM((n...  18.2 us
    unnamed x2, local copies, waits for them, and re-layouts  1.11 us

profile of v3, /device:TPU:0, one launch (start us, length us, event | category | flops | bytes accessed | tf_op | source)
XLA Modules:
  0.0 20.0 jit_solution(3573978482415107248)
XLA Ops:
  0.6 18.2 %decode_step.1 = (f32[5,16]{1,0:T(8,128)S(1)}, f32[1,16]{1,0:T(1,128)S(1)}) custom-call(bf16[16,1280]{1,0:T(8,128)(2,1)} %hidden_ref.1, bf16[384,1280]{1,0:T(8,128)(2,1)} %table_ref.1, s32[2,256]{1,0:T(2,128)} %prev_ref.1, s32[1,256]{1,0:T(1,128)} %bitcast.5, s32[1,256]{1,0:T(1,128)} %bitcast.6, s32[1,256]{1,0:T(1,128)} %bitcast.7, s32[5,256]{1,0:T(8,128)} %chosen_ref.1), custom_call_target="tpu_custom_call" | custom-call | tf_op jit(solution)/shard_map/decode_step/pallas_call | solution.py:299
  18.9 0.6 %copy.11 = f32[5,16]{1,0:T(8,128)} copy(f32[5,16]{1,0:T(8,128)S(1)} %get-tuple-element.6) | data formatting | bytes 640
  19.5 0.5 %copy.12 = f32[16]{0:T(128)} copy(f32[16]{0:T(128)S(1)} %bitcast.4) | data formatting | bytes 128

commit v4 on v3

--- a/solution.py
+++ b/solution.py
@@ -39,6 +39,7 @@
     length_in,
     chosen_in,
     ordered,
+    partial,
     stats,
     gathered,
     load_sem,
@@ -75,6 +76,14 @@
 
     load_own = pltpu.make_async_copy(hidden_ref, rows_all.at[pl.ds(pl.multiple_of(chip * row_dev, row_dev), row_dev)], load_sem.at[0])
     load_own.start()
+
+    barrier = pltpu.get_barrier_semaphore()
+    across = z * 2 + 1 - x
+    partner = chip * 2 + 1 - core
+    greeted = [(((z + i) % line) * 2 + x) * 2 + core for i in range(1, line)]
+    greeted += [across * 2 + core, partner]
+    for peer in greeted:
+        pl.semaphore_signal(barrier, inc=1, device_id=(group, peer), device_id_type=MESH)
     small = [
         pltpu.make_async_copy(source, target, load_sem.at[2 + i])
         for i, (source, target) in enumerate(
@@ -91,14 +100,6 @@
         copy.start()
     load_table = pltpu.make_async_copy(table_ref, half(core), load_sem.at[1])
     load_table.start()
-
-    barrier = pltpu.get_barrier_semaphore()
-    across = z * 2 + 1 - x
-    partner = chip * 2 + 1 - core
-    greeted = [(((z + i) % line) * 2 + x) * 2 + core for i in range(1, line)]
-    greeted += [across * 2 + core, partner]
-    for peer in greeted:
-        pl.semaphore_signal(barrier, inc=1, device_id=(group, peer), device_id_type=MESH)
 
     sends = []
 
@@ -176,23 +177,37 @@
             send(owner, part, across)
     load_table.wait()
     share.wait_recv()
+
+    def multiply(number, part):
+        at_row = number * LANES
+        if not isinstance(number, int):
+            at_row = pl.multiple_of(at_row, LANES)
+        product = lax.dot_general(
+            table[:, part * cut : (part + 1) * cut],
+            rows_all[pl.ds(at_row, LANES), part * cut : (part + 1) * cut],
+            (((1,), (1,)), ((), ())),
+            preferred_element_type=jnp.float32,
+        )
+        return product if part == 0 else product + partial[number]
+
     for part in range(parts):
         for i in [0] + order:
             arrive(((z - sign * i + 2 * line) % line) * 2 + 1 - x, part)
+        if part < parts - 1:
+
+            def add_part(number, part=part):
+                partial[number] = multiply(number, part)
+
+            if rows_half == LANES:
+                add_part(0)
+            else:
+                pl.loop(0, rows_half // LANES)(add_part)
 
     column = chip * 2 * width + lax.broadcasted_iota(jnp.int32, (2 * width, LANES), 0)
     is_text = column < stamp_begin
 
     def one_block(number):
-        at_row = number * LANES
-        if not isinstance(number, int):
-            at_row = pl.multiple_of(at_row, LANES)
-        logits = lax.dot_general(
-            table[...],
-            rows_all[pl.ds(at_row, LANES), :],
-            (((1,), (1,)), ((), ())),
-            preferred_element_type=jnp.float32,
-        )
+        logits = multiply(number, parts - 1)
         row = ordered[number]
         generated = row[4:5] - row[3:4]
         last_stamp = row[2:3]
@@ -283,6 +298,15 @@
     stamp_out_ref[...] = final[nsel : nsel + 1, :row_dev]
     for copy in stat_sends:
         copy.wait_send()
+
+
+def emit(picked_ref, stamp_ref, picked_out, stamp_out, sem):
+    first = pltpu.make_async_copy(picked_ref, picked_out, sem.at[0])
+    second = pltpu.make_async_copy(stamp_ref, stamp_out, sem.at[1])
+    first.start()
+    second.start()
+    first.wait()
+    second.wait()
 
 
 def per_device(hidden, embedding, prev_tokens, last_stamp, sample_begin, seq_length, chosen):
@@ -313,6 +337,7 @@
             pltpu.VMEM((1, rows_here), jnp.int32),
             pltpu.VMEM((nsel, rows_here), jnp.int32),
             pltpu.VMEM((rows_half // LANES, 16, LANES), jnp.int32),
+            pltpu.VMEM((rows_half // LANES, 2 * width, LANES), jnp.float32),
             pltpu.VMEM((rows_half // LANES, 8, LANES), jnp.float32),
             pltpu.VMEM((chips, 8, LANES), jnp.float32),
             pltpu.SemaphoreType.DMA((7,)),
@@ -334,6 +359,20 @@
         seq_length[None, :],
         chosen,
     )
+    picked, stamp = pl.pallas_call(
+        emit,
+        out_shape=(
+            jax.ShapeDtypeStruct((nsel, row_dev), jnp.float32),
+            jax.ShapeDtypeStruct((1, row_dev), jnp.float32),
+        ),
+        in_specs=[local, local],
+        out_specs=(anywhere, anywhere),
+        scratch_shapes=[pltpu.SemaphoreType.DMA((2,))],
+        name="emit",
+    )(
+        pltpu.with_memory_space_constraint(picked, pltpu.VMEM),
+        pltpu.with_memory_space_constraint(stamp, pltpu.VMEM),
+    )
     return picked, stamp[0]
 
 

time: 20.1 us -> 19.5 us (0.970)
  local copies, waits for them, and re-layouts: 1.11 us -> 0 us
  Pallas kernels: 18.2 us -> 18.7 us
    unnamed x2 -> x0, local copies, waits for them, and re-layouts: 1.11 us -> none
    pallas_call x0 -> x1, Pallas kernels: none -> 0.6 us  [per_device(): pl.pallas_call(emit, out_shape=(jax.ShapeDtypeStruct((nsel, row_dev), jnp...]
where the time goes in v4:
time: 19.5 us; the launch traced here: 19.4 us
  Pallas kernels  18.7 us (96%)
  between operations  0.64 us (3%)
    pallas_call x1, Pallas kernels, per_device(): pl.pallas_call(functools.partial(kernel, count), out_shape=(pltpu.VMEM((n...  18.1 us
    pallas_call x1, Pallas kernels, per_device(): pl.pallas_call(emit, out_shape=(jax.ShapeDtypeStruct((nsel, row_dev), jnp...  0.6 us

profile of v4, /device:TPU:0, one launch (start us, length us, event | category | flops | bytes accessed | tf_op | source)
XLA Modules:
  0.0 19.4 jit_solution(11233109169233704389)
XLA Ops:
  0.6 18.1 %decode_step.1 = (f32[5,16]{1,0:T(8,128)S(1)}, f32[1,16]{1,0:T(1,128)S(1)}) custom-call(bf16[16,1280]{1,0:T(8,128)(2,1)} %hidden_ref.1, bf16[384,1280]{1,0:T(8,128)(2,1)} %table_ref.1, s32[2,256]{1,0:T(2,128)} %prev_ref.1, s32[1,256]{1,0:T(1,128)} %bitcast.4, s32[1,256]{1,0:T(1,128)} %bitcast.5, s32[1,256]{1,0:T(1,128)} %bitcast.6, s32[5,256]{1,0:T(8,128)} %chosen_ref.1), custom_call_target="tpu_custom_call" | custom-call | tf_op jit(solution)/shard_map/decode_step/pallas_call | solution.py:323
  18.8 0.6 %emit.1 = (f32[5,16]{1,0:T(8,128)}, f32[1,16]{1,0:T(1,128)}) custom-call(f32[5,16]{1,0:T(8,128)S(1)} %get-tuple-element.6.picked_ref, f32[1,16]{1,0:T(1,128)S(1)} %get-tuple-element.7.stamp_ref), custom_call_target="tpu_custom_call" | custom-call | tf_op jit(solution)/shard_map/emit/pallas_call | solution.py:362

commit v5 on v4

--- a/solution.py
+++ b/solution.py
@@ -40,6 +40,7 @@
     chosen_in,
     ordered,
     partial,
+    kept,
     stats,
     gathered,
     load_sem,
@@ -178,36 +179,10 @@
     load_table.wait()
     share.wait_recv()
 
-    def multiply(number, part):
-        at_row = number * LANES
-        if not isinstance(number, int):
-            at_row = pl.multiple_of(at_row, LANES)
-        product = lax.dot_general(
-            table[:, part * cut : (part + 1) * cut],
-            rows_all[pl.ds(at_row, LANES), part * cut : (part + 1) * cut],
-            (((1,), (1,)), ((), ())),
-            preferred_element_type=jnp.float32,
-        )
-        return product if part == 0 else product + partial[number]
-
-    for part in range(parts):
-        for i in [0] + order:
-            arrive(((z - sign * i + 2 * line) % line) * 2 + 1 - x, part)
-        if part < parts - 1:
-
-            def add_part(number, part=part):
-                partial[number] = multiply(number, part)
-
-            if rows_half == LANES:
-                add_part(0)
-            else:
-                pl.loop(0, rows_half // LANES)(add_part)
-
     column = chip * 2 * width + lax.broadcasted_iota(jnp.int32, (2 * width, LANES), 0)
     is_text = column < stamp_begin
 
-    def one_block(number):
-        logits = multiply(number, parts - 1)
+    for number in range(rows_half // LANES):
         row = ordered[number]
         generated = row[4:5] - row[3:4]
         last_stamp = row[2:3]
@@ -224,7 +199,37 @@
         stamp_high = jnp.where(first, stamp_begin + INITIAL + 1, BIG)
         low = jnp.where(is_text, text_low, stamp_low)
         high = jnp.where(is_text, stamp_begin - 1, stamp_high)
-        values = jnp.where((column >= low) & (column < high), logits, MASK_VALUE)
+        kept[number] = jnp.where((column >= low) & (column < high), 1.0, 0.0)
+
+    def multiply(number, part):
+        at_row = number * LANES
+        if not isinstance(number, int):
+            at_row = pl.multiple_of(at_row, LANES)
+        product = lax.dot_general(
+            table[:, part * cut : (part + 1) * cut],
+            rows_all[pl.ds(at_row, LANES), part * cut : (part + 1) * cut],
+            (((1,), (1,)), ((), ())),
+            preferred_element_type=jnp.float32,
+        )
+        return product if part == 0 else product + partial[number]
+
+    for part in range(parts):
+        for i in [0] + order:
+            arrive(((z - sign * i + 2 * line) % line) * 2 + 1 - x, part)
+        if part < parts - 1:
+
+            def add_part(number, part=part):
+                partial[number] = multiply(number, part)
+
+            if rows_half == LANES:
+                add_part(0)
+            else:
+                pl.loop(0, rows_half // LANES)(add_part)
+
+    def one_block(number):
+        logits = multiply(number, parts - 1)
+        row = ordered[number]
+        values = jnp.where(kept[number] > 0.0, logits, MASK_VALUE)
         text_max = jnp.max(jnp.where(is_text, values, EMPTY_VALUE), axis=0, keepdims=True)
         stamp_max = jnp.max(jnp.where(is_text, EMPTY_VALUE, values), axis=0, keepdims=True)
         powers = jnp.exp(values - jnp.where(is_text, text_max, stamp_max))
@@ -338,6 +343,7 @@
             pltpu.VMEM((nsel, rows_here), jnp.int32),
             pltpu.VMEM((rows_half // LANES, 16, LANES), jnp.int32),
             pltpu.VMEM((rows_half // LANES, 2 * width, LANES), jnp.float32),
+            pltpu.VMEM((rows_half // LANES, 2 * width, LANES), jnp.float32),
             pltpu.VMEM((rows_half // LANES, 8, LANES), jnp.float32),
             pltpu.VMEM((chips, 8, LANES), jnp.float32),
             pltpu.SemaphoreType.DMA((7,)),

time: 19.5 us -> 19.5 us (level)
  no operation moved by 1% of the time
where the time goes in v5:
time: 19.5 us; the launch traced here: 19.4 us
  Pallas kernels  18.7 us (96%)
  between operations  0.64 us (3%)
    pallas_call x1, Pallas kernels, per_device(): pl.pallas_call(functools.partial(kernel, count), out_shape=(pltpu.VMEM((n...  18.1 us
    pallas_call x1, Pallas kernels, per_device(): pl.pallas_call(emit, out_shape=(jax.ShapeDtypeStruct((nsel, row_dev), jnp...  0.6 us

profile of v5, /device:TPU:0, one launch (start us, length us, event | category | flops | bytes accessed | tf_op | source)
XLA Modules:
  0.0 19.4 jit_solution(1621543828618984907)
XLA Ops:
  0.6 18.1 %decode_step.1 = (f32[5,16]{1,0:T(8,128)S(1)}, f32[1,16]{1,0:T(1,128)S(1)}) custom-call(bf16[16,1280]{1,0:T(8,128)(2,1)} %hidden_ref.1, bf16[384,1280]{1,0:T(8,128)(2,1)} %table_ref.1, s32[2,256]{1,0:T(2,128)} %prev_ref.1, s32[1,256]{1,0:T(1,128)} %bitcast.4, s32[1,256]{1,0:T(1,128)} %bitcast.5, s32[1,256]{1,0:T(1,128)} %bitcast.6, s32[5,256]{1,0:T(8,128)} %chosen_ref.1), custom_call_target="tpu_custom_call" | custom-call | tf_op jit(solution)/shard_map/decode_step/pallas_call | solution.py:328
  18.8 0.6 %emit.1 = (f32[5,16]{1,0:T(8,128)}, f32[1,16]{1,0:T(1,128)}) custom-call(f32[5,16]{1,0:T(8,128)S(1)} %get-tuple-element.6.picked_ref, f32[1,16]{1,0:T(1,128)S(1)} %get-tuple-element.7.stamp_ref), custom_call_target="tpu_custom_call" | custom-call | tf_op jit(solution)/shard_map/emit/pallas_call | solution.py:368
